TPU v7x, 32 devices: a whole 2x2x4 slice. The times are simulated.
32 devices in a mesh: ep: 4 (over y, x), fsdp: 8 (over z, core).
Axes of the slice: x: 2, y: 2, z: 4, core: 2. Of those that a mesh axis runs over, the one named last changes fastest.
Arguments:
- train_gate: float32 [64, 2048, 1408], P('ep', 'fsdp'), may hold values from -0.1875 to 0.1875
- train_up: float32 [64, 2048, 1408], P('ep', 'fsdp'), may hold values from -0.1875 to 0.1875
- train_down: float32 [64, 1408, 2048], P('ep', None, 'fsdp'), may hold values from -0.21875 to 0.21875
- router_weight: float32 [2048, 64], P('fsdp', 'ep'), may hold values from -0.125 to 0.125
- router_gain: float32 [2048], P('fsdp'), may hold values from 0.25 to 1.75
Outputs:
- ready_gate: bfloat16 [64, 2048, 1408], P('ep', None, 'fsdp')
- ready_up: bfloat16 [64, 2048, 1408], P('ep', None, 'fsdp')
- ready_down: bfloat16 [64, 1408, 2048], P('ep', 'fsdp')
- scale_gate: float32 [64, 1408], P('ep', 'fsdp')
- scale_up: float32 [64, 1408], P('ep', 'fsdp')
- scale_down: float32 [64, 1408], P('ep', 'fsdp')
- serve_router: bfloat16 [2048, 64], replicated
All inputs are finite; a program needn't handle non-finite values. Where the computation divides by a largest or mean magnitude, that divisor is 1e-20 or more.
Results may differ from a plain program's by a relative error of at most 0.001.
Values may be sent and summed in bfloat16 or wider, within the bound.
A program may use at most 256 MiB of HBM per device.

v0:
```python
import jax
import jax.numpy as jnp
from jax import lax
from jax.sharding import PartitionSpec as P


def per_device(train_gate, train_up, train_down, router_weight, router_gain):
    scale_gate, scale_up, scale_down = lax.pmax(
        (
            jnp.max(jnp.abs(train_gate), axis=1),
            jnp.max(jnp.abs(train_up), axis=1),
            jnp.max(jnp.abs(train_down), axis=2),
        ),
        "fsdp",
    )
    narrow_gate, narrow_up, narrow_down = (
        (train_gate / jnp.expand_dims(scale_gate, 1)).astype(jnp.bfloat16),
        (train_up / jnp.expand_dims(scale_up, 1)).astype(jnp.bfloat16),
        (train_down / jnp.expand_dims(scale_down, 2)).astype(jnp.bfloat16),
    )
    ready_gate, ready_up = (
        lax.all_to_all(narrow_gate, "fsdp", split_axis=2, concat_axis=1, tiled=True),
        lax.all_to_all(narrow_up, "fsdp", split_axis=2, concat_axis=1, tiled=True),
    )
    ready_down = lax.all_to_all(narrow_down, "fsdp", split_axis=1, concat_axis=2, tiled=True)
    scale_gate = lax.dynamic_slice_in_dim(
        scale_gate, lax.axis_index("fsdp") * ready_gate.shape[2], ready_gate.shape[2], axis=1
    )
    scale_up = lax.dynamic_slice_in_dim(
        scale_up, lax.axis_index("fsdp") * ready_up.shape[2], ready_up.shape[2], axis=1
    )
    scale_down = lax.dynamic_slice_in_dim(
        scale_down, lax.axis_index("fsdp") * ready_down.shape[1], ready_down.shape[1], axis=1
    )
    part_router = (router_weight * router_gain[:, None]).astype(jnp.bfloat16)
    row_router = lax.all_gather(part_router, "fsdp", axis=0, tiled=True)
    serve_router = lax.all_gather(row_router, "ep", axis=1, tiled=True)
    return (ready_gate, ready_up, ready_down, scale_gate, scale_up, scale_down, serve_router)


def solution(mesh):
    placed = (
        P("ep", "fsdp", None),
        P("ep", "fsdp", None),
        P("ep", None, "fsdp"),
        P("fsdp", "ep"),
        P("fsdp"),
    )
    return jax.shard_map(
        per_device,
        mesh=mesh,
        in_specs=placed,
        out_specs=(
            P("ep", None, "fsdp"),
            P("ep", None, "fsdp"),
            P("ep", "fsdp", None),
            P("ep", "fsdp"),
            P("ep", "fsdp"),
            P("ep", "fsdp"),
            P(),
        ),
        check_vma=False,
    )
```

profile of v0, /device:TPU:0, one launch (start us, length us, event | category | flops | bytes accessed | tf_op | source)
XLA Modules:
  0.0 985.2 jit_solution(7565016768209817902)
XLA Ops:
  7.2 0.0 all-reduce.3.cloned.1.call-start
  7.2 0.0 slice-start
  7.2 10.5 %abs_reduce_fusion = f32[16,1408]{1,0:T(8,128)} fusion(f32[16,1408,256]{2,1,0:T(8,128)} %param.7), kind=kLoop, calls=%fused_computation.2 | loop fusion | flops 11511808 | bytes 23158784 | tf_op jit(solution)/shard_map/reduce_max | solution.py:12
  17.7 10.8 %abs_reduce_fusion.1 = f32[16,1408]{1,0:T(8,128)} fusion(f32[16,256,1408]{2,1,0:T(8,128)} %param.6), kind=kLoop, calls=%fused_computation.4 | loop fusion | flops 11511808 | bytes 23158784 | tf_op jit(solution)/shard_map/reduce_max | solution.py:11
  28.6 2.4 abs_reduce_fusion.2
  31.0 0.0 all-reduce.3.cloned.1.call-update
  31.0 23.7 %copy.24 = f32[16,256,1408]{1,0,2:T(8,128)} copy(f32[16,256,1408]{2,1,0:T(8,128)} %param.5) | data formatting | bytes 46137344 | tf_op args[0]
  54.7 32.5 %all-reduce.3.cloned.1.call-done = (f32[16,1408]{1,0:T(8,128)}, f32[16,1408]{1,0:T(8,128)}, f32[16,1408]{1,0:T(8,128)}) async-done(((f32[16,1408]{1,0:T(8,128)}, f32[16,1408]{1,0:T(8,128)}, f32[16,1408]{1,0:T(8,128)}), (f32[16,1408]{1,0:T(8,128)}, f32[16,1408]{1,0:T(8,128)}, f32[16,1408]{1,0:T(8,128)})) %all-reduce.3.cloned.1.call-update) | async-done | bytes 270352 | tf_op jit(solution)/shard_map/pmax | solution.py:8
  87.2 1.1 copy.23
  88.4 14.2 %divide_convert_fusion.1 = bf16[16,256,1408]{1,0,2:T(8,128)(2,1)} fusion(f32[16,256,1408]{1,0,2:T(8,128)} %copy.24, f32[16,1408]{0,1:T(8,128)S(1)} %copy.23), kind=kLoop, calls=%fused_computation.5 | loop fusion | flops 11534336 | bytes 34693120 | tf_op jit(solution)/shard_map/convert_element_type | solution.py:17
  102.6 5.4 all-to-all-start
  108.0 23.7 %copy.28 = f32[16,256,1408]{1,0,2:T(8,128)} copy(f32[16,256,1408]{2,1,0:T(8,128)} %param.6) | data formatting | bytes 46137344 | tf_op args[1]
  131.7 0.3 copy.27
  132.0 14.2 %divide_convert_fusion = bf16[16,256,1408]{1,0,2:T(8,128)(2,1)} fusion(f32[16,256,1408]{1,0,2:T(8,128)} %copy.28, f32[16,1408]{0,1:T(8,128)S(1)} %copy.27), kind=kLoop, calls=%fused_computation.3 | loop fusion | flops 11534336 | bytes 34693120 | tf_op jit(solution)/shard_map/convert_element_type | solution.py:18
  146.2 213.1 %all-to-all-done = bf16[16,256,1408]{1,0,2:T(8,128)(2,1)} async-done(((bf16[16,256,1408]{1,0,2:T(8,128)(2,1)}), bf16[16,256,1408]{1,0,2:T(8,128)(2,1)}, u32[]{:S(2)}, u32[]{:S(2)}) %all-to-all-start) | async-done | bytes 11534368 | tf_op jit(solution)/shard_map/all_to_all | solution.py:22
  359.4 5.2 all-to-all-start.1
  364.6 0.3 copy.31
  364.9 0.0 copy-start.3
  364.9 32.6 %fusion = bf16[16,1408,256]{2,0,1:T(8,128)(2,1)} fusion(f32[16,1408,256]{2,1,0:T(8,128)} %param.7, f32[16,1408]{0,1:T(8,128)S(1)} %copy.31), kind=kLoop, calls=%fused_computation.1 | loop fusion | flops 11534336 | bytes 34693120 | tf_op jit(solution)/shard_map/convert_element_type | solution.py:19
  397.5 218.4 %all-to-all-done.1 = bf16[16,256,1408]{1,0,2:T(8,128)(2,1)} async-done(((bf16[16,256,1408]{1,0,2:T(8,128)(2,1)}), bf16[16,256,1408]{1,0,2:T(8,128)(2,1)}, u32[]{:S(2)}, u32[]{:S(2)}) %all-to-all-start.1) | async-done | bytes 11534368 | tf_op jit(solution)/shard_map/all_to_all | solution.py:23
  615.9 5.3 all-to-all-start.2
  621.3 257.3 %all_gather.6 = bf16[2048,16]{0,1:T(8,128)(2,1)S(1)} all-gather(bf16[256,16]{0,1:T(8,128)(2,1)S(1)} %multiply_convert_fusion), channel_id=1, replica_groups=mesh['ep'=4,'fsdp'=8] {'fsdp'}, dimensions={0}, use_global_device_ids=true | all-gather | bytes 73728 | tf_op jit(solution)/shard_map/all_gather | solution.py:36
  878.5 9.1 all_gather.7
  887.7 1.4 constant_dynamic-slice_fusion.2
  889.1 0.7 constant_dynamic-slice_fusion
  889.8 11.3 %copy.26 = bf16[16,8,256,176]{2,1,3,0:T(8,128)(2,1)} copy(bf16[16,8,256,176]{2,0,3,1:T(8,128)(2,1)} %bitcast.2) | data formatting | bytes 23068672 | tf_op jit(solution)/shard_map/all_to_all | solution.py:22
  901.1 18.0 %all_to_all.42 = bf16[16,2048,176]{1,2,0:T(8,128)(2,1)} reshape(bf16[16,8,256,176]{2,1,3,0:T(8,128)(2,1)} %copy.26) | data formatting | bytes 23068672 | tf_op jit(solution)/shard_map/all_to_all | solution.py:22
  919.1 11.3 %copy.30 = bf16[16,8,256,176]{2,1,3,0:T(8,128)(2,1)} copy(bf16[16,8,256,176]{2,0,3,1:T(8,128)(2,1)} %bitcast.5) | data formatting | bytes 23068672 | tf_op jit(solution)/shard_map/all_to_all | solution.py:23
  930.4 18.0 %all_to_all.46 = bf16[16,2048,176]{1,2,0:T(8,128)(2,1)} reshape(bf16[16,8,256,176]{2,1,3,0:T(8,128)(2,1)} %copy.30) | data formatting | bytes 23068672 | tf_op jit(solution)/shard_map/all_to_all | solution.py:23
  948.4 11.4 %copy.33 = bf16[16,176,8,256]{3,2,1,0:T(8,128)(2,1)} copy(bf16[16,176,8,256]{3,0,1,2:T(8,128)(2,1)} %bitcast.7) | data formatting | bytes 23068672 | tf_op jit(solution)/shard_map/all_to_all | solution.py:25
  959.7 18.0 %all_to_all.50 = bf16[16,176,2048]{2,1,0:T(8,128)(2,1)} reshape(bf16[16,176,8,256]{3,2,1,0:T(8,128)(2,1)} %copy.33) | data formatting | bytes 23068672 | tf_op jit(solution)/shard_map/all_to_all | solution.py:25
  977.7 0.7 copy.43
  (21 shorter events, 0.0 us)
Async XLA Ops:
  7.2 80.1 %all-reduce.3.cloned.1.call-start = ((), (), s32[]{:S(2)}) async-start(), calls=%async_computation.3 | async-start | bytes 540672 | tf_op jit(solution)/shard_map/pmax | solution.py:8
  7.2 21.3 %slice-start = ((s8[23068672]{0:T(1024)(128)(4,1)}), s8[4194304]{0:T(1024)(128)(4,1)S(1)}, s32[]{:S(2)}) async-start(s8[23068672]{0:T(1024)(128)(4,1)} %bitcast.19), calls=%async_computation.4 | async-start | bytes 8388608
  7.2 21.3 %slice-start.1 = ((s8[23068672]{0:T(1024)(128)(4,1)}), s8[4194304]{0:T(1024)(128)(4,1)S(1)}, s32[]{:S(2)}) async-start(s8[23068672]{0:T(1024)(128)(4,1)} %bitcast.19), calls=%async_computation.5 | async-start | bytes 8388608
  7.2 21.3 %slice-start.2 = ((s8[23068672]{0:T(1024)(128)(4,1)}), s8[4194304]{0:T(1024)(128)(4,1)S(1)}, s32[]{:S(2)}) async-start(s8[23068672]{0:T(1024)(128)(4,1)} %bitcast.19), calls=%async_computation.6 | async-start | bytes 8388608
  17.7 10.8 %slice-start.3 = ((s8[23068672]{0:T(1024)(128)(4,1)}), s8[4194304]{0:T(1024)(128)(4,1)S(1)}, s32[]{:S(2)}) async-start(s8[23068672]{0:T(1024)(128)(4,1)} %bitcast.19), calls=%async_computation.7 | async-start | bytes 8388608
  17.7 10.8 %slice-start.4 = ((s8[23068672]{0:T(1024)(128)(4,1)}), s8[4194304]{0:T(1024)(128)(4,1)S(1)}, s32[]{:S(2)}) async-start(s8[23068672]{0:T(1024)(128)(4,1)} %bitcast.19), calls=%async_computation.8 | async-start | bytes 8388608
  17.7 10.9 %slice-start.5 = ((s8[23068672]{0:T(1024)(128)(4,1)}), s8[2097152]{0:T(1024)(128)(4,1)S(1)}, s32[]{:S(2)}) async-start(s8[23068672]{0:T(1024)(128)(4,1)} %bitcast.19), calls=%async_computation.9 | async-start | bytes 4194304
  102.6 256.8 %all-to-all-start = ((bf16[16,256,1408]{1,0,2:T(8,128)(2,1)}), bf16[16,256,1408]{1,0,2:T(8,128)(2,1)}, u32[]{:S(2)}, u32[]{:S(2)}) async-start(bf16[16,256,1408]{1,0,2:T(8,128)(2,1)} %divide_convert_fusion.1), calls=%async_computation | async-start | bytes 23068672 | tf_op jit(solution)/shard_map/all_to_all | solution.py:22
  108.0 23.7 %copy-start = (f32[16,1408]{1,0:T(8,128)S(1)}, f32[16,1408]{1,0:T(8,128)}, u32[]{:S(2)}) copy-start(f32[16,1408]{1,0:T(8,128)} %get-tuple-element.8) | copy-start | bytes 270340
  132.0 232.6 %copy-start.1 = (f32[16,1408]{1,0:T(8,128)S(1)}, f32[16,1408]{1,0:T(8,128)}, u32[]{:S(2)}) copy-start(f32[16,1408]{1,0:T(8,128)} %get-tuple-element.9) | copy-start | bytes 270340
  359.4 256.5 %all-to-all-start.1 = ((bf16[16,256,1408]{1,0,2:T(8,128)(2,1)}), bf16[16,256,1408]{1,0,2:T(8,128)(2,1)}, u32[]{:S(2)}, u32[]{:S(2)}) async-start(bf16[16,256,1408]{1,0,2:T(8,128)(2,1)} %divide_convert_fusion), calls=%async_computation.1 | async-start | bytes 23068672 | tf_op jit(solution)/shard_map/all_to_all | solution.py:23
  364.9 256.3 %copy-start.2 = (f32[256,16]{0,1:T(8,128)S(1)}, f32[256,16]{0,1:T(8,128)}, u32[]{:S(2)}) copy-start(f32[256,16]{0,1:T(8,128)} %param.8) | copy-start | bytes 49156
  364.9 256.3 %copy-start.3 = (f32[256]{0:T(256)S(1)}, f32[256]{0:T(256)}, u32[]{:S(2)}) copy-start(f32[256]{0:T(256)} %param.9) | copy-start | bytes 3076
  615.9 332.5 %all-to-all-start.2 = ((bf16[16,1408,256]{2,0,1:T(8,128)(2,1)}), bf16[16,1408,256]{2,0,1:T(8,128)(2,1)}, u32[]{:S(2)}, u32[]{:S(2)}) async-start(bf16[16,1408,256]{2,0,1:T(8,128)(2,1)} %fusion), calls=%async_computation.2 | async-start | bytes 23068672 | tf_op jit(solution)/shard_map/all_to_all | solution.py:25
Sparse Core Ops, SparseCore 0:
  31.1 56.0 all-reduce.2
where the time goes:
time: 988 us; the launch traced here: 985 us
  waiting for transfers between devices  464 us (47%)
  blocking collectives  266 us (27%)
  local copies, waits for them, and re-layouts  140 us (14%)
  other arithmetic  84.8 us (9%)
  starting transfers between devices  16 us (2%)
  between operations  14.2 us (1%)
    all_gather x1, blocking collectives, per_device(): row_router = lax.all_gather(part_router, 'fsdp', axis=0, tiled=True)  257 us
    all_to_all x1, waiting for transfers between devices, per_device(): lax.all_to_all(narrow_up, 'fsdp', split_axis=2, concat_axis=1, tiled=True)  218 us
    all_to_all x1, waiting for transfers between devices, per_device(): lax.all_to_all(narrow_gate, 'fsdp', split_axis=2, concat_axis=1, tiled=True)  213 us
    unnamed x23, local copies, waits for them, and re-layouts  48.2 us
    convert_element_type x1, other arithmetic, per_device(): (train_down / jnp.expand_dims(scale_down, 2)).astype(jnp.bfloat16)  32.6 us
    pmax x1, waiting for transfers between devices, per_device(): lax.pmax((jnp.max(jnp.abs(train_gate), axis=1), jnp.max(jnp.abs(train_up)...  32.5 us
    all_to_all x2, local copies, waits for them, and re-layouts, per_device(): lax.all_to_all(narrow_down, 'fsdp', split_axis=1, concat_axis=2, tiled=True)  29.3 us
    all_to_all x2, local copies, waits for them, and re-layouts, per_device(): lax.all_to_all(narrow_gate, 'fsdp', split_axis=2, concat_axis=1, tiled=True)  29.3 us
  transfers between devices with their start and end apart: 4, of which 3 were waited for; matrix products, arithmetic and copies ran while one was open for 12% of the time, Pallas kernels for 0%

commit v1 on v0

--- a/solution.py
+++ b/solution.py
@@ -34,7 +34,7 @@
     )
     part_router = (router_weight * router_gain[:, None]).astype(jnp.bfloat16)
     row_router = lax.all_gather(part_router, "fsdp", axis=0, tiled=True)
-    serve_router = lax.all_gather(row_router, "ep", axis=1, tiled=True)
+    serve_router = jnp.concatenate(lax.all_gather(row_router, "ep"), axis=1)
     return (ready_gate, ready_up, ready_down, scale_gate, scale_up, scale_down, serve_router)
 
 

time: 988 us -> 988 us (level)
    unnamed x23 -> x22, local copies, waits for them, and re-layouts: 48.2 us -> 47.5 us
where the time goes in v1:
time: 988 us; the launch traced here: 985 us
  waiting for transfers between devices  464 us (47%)
  blocking collectives  266 us (27%)
  local copies, waits for them, and re-layouts  140 us (14%)
  other arithmetic  84.8 us (9%)
  starting transfers between devices  16 us (2%)
  between operations  14.2 us (1%)
    all_gather x1, blocking collectives, per_device(): row_router = lax.all_gather(part_router, 'fsdp', axis=0, tiled=True)  257 us
    all_to_all x1, waiting for transfers between devices, per_device(): lax.all_to_all(narrow_up, 'fsdp', split_axis=2, concat_axis=1, tiled=True)  218 us
    all_to_all x1, waiting for transfers between devices, per_device(): lax.all_to_all(narrow_gate, 'fsdp', split_axis=2, concat_axis=1, tiled=True)  213 us
    unnamed x22, local copies, waits for them, and re-layouts  47.5 us
    convert_element_type x1, other arithmetic, per_device(): (train_down / jnp.expand_dims(scale_down, 2)).astype(jnp.bfloat16)  32.6 us
    pmax x1, waiting for transfers between devices, per_device(): lax.pmax((jnp.max(jnp.abs(train_gate), axis=1), jnp.max(jnp.abs(train_up)...  32.5 us
    all_to_all x2, local copies, waits for them, and re-layouts, per_device(): lax.all_to_all(narrow_down, 'fsdp', split_axis=1, concat_axis=2, tiled=True)  29.3 us
    all_to_all x2, local copies, waits for them, and re-layouts, per_device(): lax.all_to_all(narrow_gate, 'fsdp', split_axis=2, concat_axis=1, tiled=True)  29.3 us
  transfers between devices with their start and end apart: 4, of which 3 were waited for; matrix products, arithmetic and copies ran while one was open for 12% of the time, Pallas kernels for 0%

profile of v1, /device:TPU:0, one launch (start us, length us, event | category | flops | bytes accessed | tf_op | source)
XLA Modules:
  0.0 985.3 jit_solution(11771086698281584803)
XLA Ops:
  7.2 0.0 all-reduce.3.cloned.1.call-start
  7.2 0.0 slice-start
  7.2 10.5 %abs_reduce_fusion = f32[16,1408]{1,0:T(8,128)} fusion(f32[16,1408,256]{2,1,0:T(8,128)} %param.7), kind=kLoop, calls=%fused_computation.2 | loop fusion | flops 11511808 | bytes 23158784 | tf_op jit(solution)/shard_map/reduce_max | solution.py:12
  17.7 10.8 %abs_reduce_fusion.1 = f32[16,1408]{1,0:T(8,128)} fusion(f32[16,256,1408]{2,1,0:T(8,128)} %param.6), kind=kLoop, calls=%fused_computation.4 | loop fusion | flops 11511808 | bytes 23158784 | tf_op jit(solution)/shard_map/reduce_max | solution.py:11
  28.6 2.4 abs_reduce_fusion.2
  31.0 0.0 all-reduce.3.cloned.1.call-update
  31.0 23.7 %copy.27 = f32[16,256,1408]{1,0,2:T(8,128)} copy(f32[16,256,1408]{2,1,0:T(8,128)} %param.5) | data formatting | bytes 46137344 | tf_op args[0]
  54.7 32.5 %all-reduce.3.cloned.1.call-done = (f32[16,1408]{1,0:T(8,128)}, f32[16,1408]{1,0:T(8,128)}, f32[16,1408]{1,0:T(8,128)}) async-done(((f32[16,1408]{1,0:T(8,128)}, f32[16,1408]{1,0:T(8,128)}, f32[16,1408]{1,0:T(8,128)}), (f32[16,1408]{1,0:T(8,128)}, f32[16,1408]{1,0:T(8,128)}, f32[16,1408]{1,0:T(8,128)})) %all-reduce.3.cloned.1.call-update) | async-done | bytes 270352 | tf_op jit(solution)/shard_map/pmax | solution.py:8
  87.2 1.1 copy.26
  88.4 14.2 %divide_convert_fusion.1 = bf16[16,256,1408]{1,0,2:T(8,128)(2,1)} fusion(f32[16,256,1408]{1,0,2:T(8,128)} %copy.27, f32[16,1408]{0,1:T(8,128)S(1)} %copy.26), kind=kLoop, calls=%fused_computation.5 | loop fusion | flops 11534336 | bytes 34693120 | tf_op jit(solution)/shard_map/convert_element_type | solution.py:17
  102.6 5.4 all-to-all-start
  108.0 23.7 %copy.31 = f32[16,256,1408]{1,0,2:T(8,128)} copy(f32[16,256,1408]{2,1,0:T(8,128)} %param.6) | data formatting | bytes 46137344 | tf_op args[1]
  131.7 0.3 copy.30
  132.0 14.2 %divide_convert_fusion = bf16[16,256,1408]{1,0,2:T(8,128)(2,1)} fusion(f32[16,256,1408]{1,0,2:T(8,128)} %copy.31, f32[16,1408]{0,1:T(8,128)S(1)} %copy.30), kind=kLoop, calls=%fused_computation.3 | loop fusion | flops 11534336 | bytes 34693120 | tf_op jit(solution)/shard_map/convert_element_type | solution.py:18
  146.2 213.1 %all-to-all-done = bf16[16,256,1408]{1,0,2:T(8,128)(2,1)} async-done(((bf16[16,256,1408]{1,0,2:T(8,128)(2,1)}), bf16[16,256,1408]{1,0,2:T(8,128)(2,1)}, u32[]{:S(2)}, u32[]{:S(2)}) %all-to-all-start) | async-done | bytes 11534368 | tf_op jit(solution)/shard_map/all_to_all | solution.py:22
  359.4 5.2 all-to-all-start.1
  364.6 0.3 copy.34
  364.9 0.0 copy-start.3
  364.9 32.6 %fusion = bf16[16,1408,256]{2,0,1:T(8,128)(2,1)} fusion(f32[16,1408,256]{2,1,0:T(8,128)} %param.7, f32[16,1408]{0,1:T(8,128)S(1)} %copy.34), kind=kLoop, calls=%fused_computation.1 | loop fusion | flops 11534336 | bytes 34693120 | tf_op jit(solution)/shard_map/convert_element_type | solution.py:19
  397.5 218.4 %all-to-all-done.1 = bf16[16,256,1408]{1,0,2:T(8,128)(2,1)} async-done(((bf16[16,256,1408]{1,0,2:T(8,128)(2,1)}), bf16[16,256,1408]{1,0,2:T(8,128)(2,1)}, u32[]{:S(2)}, u32[]{:S(2)}) %all-to-all-start.1) | async-done | bytes 11534368 | tf_op jit(solution)/shard_map/all_to_all | solution.py:23
  615.9 5.3 all-to-all-start.2
  621.3 257.3 %all_gather.9 = bf16[2048,16]{0,1:T(8,128)(2,1)S(1)} all-gather(bf16[256,16]{0,1:T(8,128)(2,1)S(1)} %multiply_convert_fusion), channel_id=1, replica_groups=mesh['ep'=4,'fsdp'=8] {'fsdp'}, dimensions={0}, use_global_device_ids=true | all-gather | bytes 73728 | tf_op jit(solution)/shard_map/all_gather | solution.py:36
  878.5 9.1 all-gather
  887.7 0.7 copy.45
  888.4 1.4 constant_dynamic-slice_fusion.2
  889.8 0.7 constant_dynamic-slice_fusion
  890.5 11.3 %copy.29 = bf16[16,8,256,176]{2,1,3,0:T(8,128)(2,1)} copy(bf16[16,8,256,176]{2,0,3,1:T(8,128)(2,1)} %bitcast.2) | data formatting | bytes 23068672 | tf_op jit(solution)/shard_map/all_to_all | solution.py:22
  901.8 18.0 %all_to_all.42 = bf16[16,2048,176]{1,2,0:T(8,128)(2,1)} reshape(bf16[16,8,256,176]{2,1,3,0:T(8,128)(2,1)} %copy.29) | data formatting | bytes 23068672 | tf_op jit(solution)/shard_map/all_to_all | solution.py:22
  919.8 11.3 %copy.33 = bf16[16,8,256,176]{2,1,3,0:T(8,128)(2,1)} copy(bf16[16,8,256,176]{2,0,3,1:T(8,128)(2,1)} %bitcast.5) | data formatting | bytes 23068672 | tf_op jit(solution)/shard_map/all_to_all | solution.py:23
  931.1 18.0 %all_to_all.46 = bf16[16,2048,176]{1,2,0:T(8,128)(2,1)} reshape(bf16[16,8,256,176]{2,1,3,0:T(8,128)(2,1)} %copy.33) | data formatting | bytes 23068672 | tf_op jit(solution)/shard_map/all_to_all | solution.py:23
  949.1 11.4 %copy.36 = bf16[16,176,8,256]{3,2,1,0:T(8,128)(2,1)} copy(bf16[16,176,8,256]{3,0,1,2:T(8,128)(2,1)} %bitcast.7) | data formatting | bytes 23068672 | tf_op jit(solution)/shard_map/all_to_all | solution.py:25
  960.4 18.0 %all_to_all.50 = bf16[16,176,2048]{2,1,0:T(8,128)(2,1)} reshape(bf16[16,176,8,256]{3,2,1,0:T(8,128)(2,1)} %copy.36) | data formatting | bytes 23068672 | tf_op jit(solution)/shard_map/all_to_all | solution.py:25
  (21 shorter events, 0.0 us)
Async XLA Ops:
  7.2 80.1 %all-reduce.3.cloned.1.call-start = ((), (), s32[]{:S(2)}) async-start(), calls=%async_computation.3 | async-start | bytes 540672 | tf_op jit(solution)/shard_map/pmax | solution.py:8
  7.2 21.3 %slice-start = ((s8[23068672]{0:T(1024)(128)(4,1)}), s8[4194304]{0:T(1024)(128)(4,1)S(1)}, s32[]{:S(2)}) async-start(s8[23068672]{0:T(1024)(128)(4,1)} %bitcast.26), calls=%async_computation.4 | async-start | bytes 8388608
  7.2 21.3 %slice-start.1 = ((s8[23068672]{0:T(1024)(128)(4,1)}), s8[4194304]{0:T(1024)(128)(4,1)S(1)}, s32[]{:S(2)}) async-start(s8[23068672]{0:T(1024)(128)(4,1)} %bitcast.26), calls=%async_computation.5 | async-start | bytes 8388608
  7.2 21.3 %slice-start.2 = ((s8[23068672]{0:T(1024)(128)(4,1)}), s8[4194304]{0:T(1024)(128)(4,1)S(1)}, s32[]{:S(2)}) async-start(s8[23068672]{0:T(1024)(128)(4,1)} %bitcast.26), calls=%async_computation.6 | async-start | bytes 8388608
  17.7 10.8 %slice-start.3 = ((s8[23068672]{0:T(1024)(128)(4,1)}), s8[4194304]{0:T(1024)(128)(4,1)S(1)}, s32[]{:S(2)}) async-start(s8[23068672]{0:T(1024)(128)(4,1)} %bitcast.26), calls=%async_computation.7 | async-start | bytes 8388608
  17.7 10.8 %slice-start.4 = ((s8[23068672]{0:T(1024)(128)(4,1)}), s8[4194304]{0:T(1024)(128)(4,1)S(1)}, s32[]{:S(2)}) async-start(s8[23068672]{0:T(1024)(128)(4,1)} %bitcast.26), calls=%async_computation.8 | async-start | bytes 8388608
  17.7 10.9 %slice-start.5 = ((s8[23068672]{0:T(1024)(128)(4,1)}), s8[2097152]{0:T(1024)(128)(4,1)S(1)}, s32[]{:S(2)}) async-start(s8[23068672]{0:T(1024)(128)(4,1)} %bitcast.26), calls=%async_computation.9 | async-start | bytes 4194304
  102.6 256.8 %all-to-all-start = ((bf16[16,256,1408]{1,0,2:T(8,128)(2,1)}), bf16[16,256,1408]{1,0,2:T(8,128)(2,1)}, u32[]{:S(2)}, u32[]{:S(2)}) async-start(bf16[16,256,1408]{1,0,2:T(8,128)(2,1)} %divide_convert_fusion.1), calls=%async_computation | async-start | bytes 23068672 | tf_op jit(solution)/shard_map/all_to_all | solution.py:22
  108.0 23.7 %copy-start = (f32[16,1408]{1,0:T(8,128)S(1)}, f32[16,1408]{1,0:T(8,128)}, u32[]{:S(2)}) copy-start(f32[16,1408]{1,0:T(8,128)} %get-tuple-element.8) | copy-start | bytes 270340
  132.0 232.6 %copy-start.1 = (f32[16,1408]{1,0:T(8,128)S(1)}, f32[16,1408]{1,0:T(8,128)}, u32[]{:S(2)}) copy-start(f32[16,1408]{1,0:T(8,128)} %get-tuple-element.9) | copy-start | bytes 270340
  359.4 256.5 %all-to-all-start.1 = ((bf16[16,256,1408]{1,0,2:T(8,128)(2,1)}), bf16[16,256,1408]{1,0,2:T(8,128)(2,1)}, u32[]{:S(2)}, u32[]{:S(2)}) async-start(bf16[16,256,1408]{1,0,2:T(8,128)(2,1)} %divide_convert_fusion), calls=%async_computation.1 | async-start | bytes 23068672 | tf_op jit(solution)/shard_map/all_to_all | solution.py:23
  364.9 256.3 %copy-start.2 = (f32[256,16]{0,1:T(8,128)S(1)}, f32[256,16]{0,1:T(8,128)}, u32[]{:S(2)}) copy-start(f32[256,16]{0,1:T(8,128)} %param.8) | copy-start | bytes 49156
  364.9 256.3 %copy-start.3 = (f32[256]{0:T(256)S(1)}, f32[256]{0:T(256)}, u32[]{:S(2)}) copy-start(f32[256]{0:T(256)} %param.9) | copy-start | bytes 3076
  615.9 333.2 %all-to-all-start.2 = ((bf16[16,1408,256]{2,0,1:T(8,128)(2,1)}), bf16[16,1408,256]{2,0,1:T(8,128)(2,1)}, u32[]{:S(2)}, u32[]{:S(2)}) async-start(bf16[16,1408,256]{2,0,1:T(8,128)(2,1)} %fusion), calls=%async_computation.2 | async-start | bytes 23068672 | tf_op jit(solution)/shard_map/all_to_all | solution.py:25
Sparse Core Ops, SparseCore 0:
  31.1 56.0 all-reduce.2
